TPU v7x, 256 devices: a 4x2x16 block of a 4x16x16 slice. The times are simulated.
256 devices in a mesh: pb: 2 (over y), band: 128 (over z, x, core).
Axes of the slice: x: 4, y: 2, z: 16, core: 2. Of those that a mesh axis runs over, the one named last changes fastest.
The devices are a block of a 4x16x16 slice.
Arguments:
- wavefunctions: bfloat16 [2, 64, 16384], P(None, None, 'band'), may hold values from -6 to 6
- k_vectors: float32 [3, 16384], P(None, 'band'), may hold values from -2 to 2
- beta_k: bfloat16 [2, 16384, 3072], P(None, 'band'), may hold values from -0.03125 to 0.03125
- beta_kq: bfloat16 [2, 32768, 3072], P(None, ('pb', 'band')), parts along dimension 1, may hold values from -0.078125 to 0.078125
- kq_vectors: float32 [3, 32768], P(None, ('pb', 'band')), parts along dimension 1, may hold values from -2 to 2
- d_matrix: float32 [4, 8, 8], replicated, may hold values from -2.1 to 2.1
- species: int32 [384], replicated, may hold values from 0 to 3
- displacements: float32 [6, 384, 3], P('pb'), parts along dimension 0, may hold values from -6 to 6
Outputs:
- response: bfloat16 [6, 2, 64, 16384], P('pb', None, None, 'band'), parts along dimension 0
There are 2 independent parts, one for each index of `pb`. A program takes and returns all parts, laid end to end along the dimension named above; an argument that names none is the same for every part. Nothing has to cross between parts.
All inputs are finite; a program needn't handle non-finite values.
Results may differ from a plain program's by a relative error of at most 0.0054.
Values sent between devices are 32-bit elements; how exact they have to be, the bound alone decides.
A program may use at most 128 MiB of HBM per device.

v0:
```python
import jax
import jax.numpy as jnp
from jax import lax
from jax.sharding import PartitionSpec as P


def scaled_columns(waves, k_vectors):
    waves_f = waves.astype(jnp.float32)
    moved = waves_f[:, None, :, :] * k_vectors[None, :, None, :]
    stacked = jnp.concatenate([waves_f[:, None], moved], axis=1).astype(jnp.bfloat16)
    band_count = waves.shape[1]
    wave_count = waves.shape[2]
    real_part = stacked[0].reshape(4 * band_count, wave_count)
    imag_part = stacked[1].reshape(4 * band_count, wave_count)
    return jnp.stack(
        [jnp.concatenate([real_part, imag_part], 0), jnp.concatenate([imag_part, -real_part], 0)]
    )


def atom_matrices(species, d_matrix):
    kinds = jnp.arange(d_matrix.shape[0], dtype=jnp.int32)
    onehot = (species[:, None] == kinds[None, :]).astype(jnp.float32)
    per_atom = d_matrix.shape[1]
    flat = jnp.dot(
        onehot,
        d_matrix.reshape(d_matrix.shape[0], per_atom * per_atom),
        precision=lax.Precision.HIGHEST,
    )
    return flat.reshape(species.shape[0], per_atom, per_atom)


def apply_dmat(block, atom_mats):
    shaped = block.reshape(atom_mats.shape[0], atom_mats.shape[1], block.shape[1])
    mixed = jnp.einsum("aij,ajc->aic", atom_mats, shaped, precision=lax.Precision.HIGHEST)
    return mixed.reshape(block.shape)


def coefficients(dcols, modes_part, per_atom):
    row_count = dcols.shape[0]
    band_count = dcols.shape[1] // 8
    pieces = dcols.reshape(row_count, 2, 4, band_count)
    weights = jnp.repeat(modes_part, per_atom, axis=1)
    turned_real = jnp.einsum(
        "mpa,pab->mpb", weights, pieces[:, 0, 1:], precision=lax.Precision.HIGHEST
    )
    turned_imag = jnp.einsum(
        "mpa,pab->mpb", weights, pieces[:, 1, 1:], precision=lax.Precision.HIGHEST
    )
    plain_real = weights[:, :, :, None] * pieces[None, :, 0, 0][:, :, None, :]
    plain_imag = weights[:, :, :, None] * pieces[None, :, 1, 0][:, :, None, :]
    real_part = jnp.concatenate([-turned_imag[:, :, None], plain_real], axis=2)
    imag_part = jnp.concatenate([turned_real[:, :, None], plain_imag], axis=2)
    real_part = (
        real_part.transpose(1, 0, 2, 3).reshape(row_count, 12 * band_count).astype(jnp.bfloat16)
    )
    imag_part = (
        imag_part.transpose(1, 0, 2, 3).reshape(row_count, 12 * band_count).astype(jnp.bfloat16)
    )
    return jnp.stack(
        [jnp.concatenate([real_part, imag_part], 1), jnp.concatenate([-imag_part, real_part], 1)]
    )


def project_back(coef, beta_cols):
    return lax.dot_general(
        coef, beta_cols, (((0, 1), (0, 2)), ((), ())), preferred_element_type=jnp.float32
    )


def finish(back, kq_vectors, band_count):
    pieces = back.reshape(2, 3, 4, band_count, back.shape[1])
    back_real = pieces[0]
    back_imag = pieces[1]
    shifted = kq_vectors[None, :, None, :]
    out_real = back_real[:, 0] + jnp.sum(shifted * back_imag[:, 1:], axis=1)
    out_imag = back_imag[:, 0] - jnp.sum(shifted * back_real[:, 1:], axis=1)
    return jnp.stack([out_real, out_imag], 1).astype(jnp.bfloat16)


def body(wavefunctions, k_vectors, beta_k, beta_kq, kq_vectors, d_matrix, species, displacements):
    per_atom = d_matrix.shape[1]
    band_count = wavefunctions.shape[1]
    right = scaled_columns(wavefunctions, k_vectors)
    partial_value = lax.dot_general(
        beta_k, right, (((0, 1), (0, 2)), ((), ())), preferred_element_type=jnp.float32
    )
    atom_mats = atom_matrices(species, d_matrix)
    summed = lax.psum(partial_value, "band")
    dcols = apply_dmat(summed, atom_mats)
    coef = coefficients(dcols, displacements, per_atom)
    back = project_back(coef, beta_kq)
    return finish(back, kq_vectors, band_count)


def solution(mesh):
    in_specs = (
        P(None, None, "band"),
        P(None, "band"),
        P(None, "band", None),
        P(None, ("pb", "band"), None),
        P(None, ("pb", "band")),
        P(),
        P(),
        P("pb", None, None),
    )
    out_specs = P("pb", None, None, "band")
    return jax.shard_map(body, mesh=mesh, in_specs=in_specs, out_specs=out_specs, check_vma=False)
```

profile of v0, /device:TPU:33, one launch (start us, length us, event | category | flops | bytes accessed | tf_op | source)
XLA Modules:
  0.0 504.9 jit_solution(8847159657788263222)
XLA Ops:
  6.6 0.9 convert_element_type.20
  7.4 0.7 multiply_convert_fusion.2
  8.1 0.8 pad_maximum_fusion.3
  9.0 3.6 convolution_bitcast_fusion
  12.6 6.5 %copy.20 = f32[3072,512]{1,0:T(8,128)} copy(f32[3072,512]{0,1:T(8,128)} %convolution_bitcast_fusion) | data formatting | bytes 12582912 | tf_op jit(solution)/shard_map/dot_general | solution.py:84
  19.1 0.1 all-reduce.2.cloned.1.call-update
  19.2 0.6 copy-done.6
  19.9 0.1 reshape.31
  19.9 0.1 dot_general.25
  20.0 0.3 copy.22
  20.4 0.3 fusion.16
  20.7 0.6 copy.30
  21.3 3.4 broadcast_in_dim.18
  24.7 5.6 %copy.23 = f32[3,3072,3]{1,2,0:T(4,128)} copy(f32[3,3072,3]{2,0,1:T(4,128)} %bitcast.71) | data formatting | bytes 221184 | tf_op jit(solution)/shard_map/reshape | solution.py:42
  30.3 362.0 %all-reduce.2.cloned.1.call-done = f32[384,8,512]{2,1,0:T(8,128)} async-done(((f32[384,8,512]{2,1,0:T(8,128)}), f32[384,8,512]{2,1,0:T(8,128)}) %all-reduce.2.cloned.1.call-update) | async-done | bytes 6291472 | tf_op jit(solution)/shard_map/psum | solution.py:88
  392.2 9.1 %fusion.27 = f32[384,8,512]{2,1,0:T(8,128)} fusion(f32[384,8,8]{2,1,0:T(8,128)S(1)} %copy.30, f32[384,8,512]{2,1,0:T(8,128)} %all-reduce.2.cloned.1.call-done), kind=kOutput, calls=%fused_computation.49 | convolution fusion | flops 150994944 | bytes 12681216 | tf_op jit(solution)/shard_map/aij,ajc->aic/dot_general | solution.py:34
  401.3 12.3 %reshape_reshape.3 = f32[3072,2,4,64]{3,2,1,0:T(4,128)} reshape(f32[384,8,512]{2,1,0:T(8,128)} %fusion.27) | data formatting | bytes 12582912 | tf_op jit(solution)/shard_map/reshape;reshape | solution.py:41
  413.7 25.2 %fusion.6 = bf16[3,3072,1,64]{3,0,1,2:T(4,128)(2,1)} fusion(f32[3,3072,3]{2,0,1:T(4,128)} %bitcast.72, f32[3072,2,4,64]{3,2,1,0:T(4,128)} %reshape_reshape.3), kind=kOutput, calls=%fused_computation.16 | convolution fusion | flops 22413312 | bytes 13762560 | tf_op jit(solution)/shard_map/mpa,pab->mpb/dot_general | solution.py:46
  438.9 24.5 %convert_bitcast_fusion = bf16[3,3072,1,64]{3,0,1,2:T(4,128)(2,1)} fusion(f32[3,3072,3]{2,0,1:T(4,128)} %bitcast.73, f32[3072,2,4,64]{3,2,1,0:T(4,128)S(1)} %copy-done.2), kind=kOutput, calls=%fused_computation.17 | convolution fusion | flops 21823488 | bytes 7581696 | tf_op jit(solution)/shard_map/mpa,pab->mpb/dot_general | solution.py:43
  463.4 2.2 fusion.25
  465.6 5.0 copy.28
  470.5 5.0 copy.25
  475.5 1.3 copy.27
  476.8 0.4 copy.24
  477.3 2.9 multiply_convert_fusion
  480.2 0.9 pad_maximum_fusion
  481.1 0.6 bitcast_negate_fusion
  481.7 0.0 copy-start.8
  481.7 7.8 %maximum_bitcast_fusion = (bf16[1,3072,1536]{1,2,0:T(8,128)(2,1)S(1)}, bf16[1,3072,1536]{1,2,0:T(8,128)(2,1)}) fusion(bf16[3072,768]{0,1:T(8,128)(2,1)S(1)} %bitcast.74, bf16[3072,768]{0,1:T(8,128)(2,1)S(1)} %bitcast.76, bf16[3072,768]{0,1:T(8,128)(2,1)S(1)} %bitcast_negate_fusion), kind=kLoop, calls=%fused_computation.4 | loop fusion | flops 37748736 | bytes 33030144 | tf_op jit(solution)/shard_map/stack | solution.py:59
  489.5 7.7 %fusion.7 = f32[1536,128]{1,0:T(8,128)S(1)} fusion(bf16[2,128,3072]{2,1,0:T(8,128)(2,1)S(1)} %copy-done.8, bf16[1,3072,1536]{1,2,0:T(8,128)(2,1)} %get-tuple-element.10, bf16[1,3072,1536]{1,2,0:T(8,128)(2,1)S(1)} %get-tuple-element.9), kind=kOutput, calls=%fused_computation.18 | convolution fusion | flops 2425356288 | bytes 21233664 | tf_op jit(solution)/shard_map/dot_general | solution.py:65
  497.2 0.1 fusion.26
  497.4 0.7 pad_maximum_fusion.2
  (24 shorter events, 0.1 us)
Async XLA Ops:
  6.5 2.4 copy-start
  6.6 385.7 %all-reduce.2.cloned.1.call-start = ((), (), s32[]{:S(2)}) async-start(), calls=%async_computation | async-start | bytes 12582912 | tf_op jit(solution)/shard_map/psum | solution.py:88
  19.1 0.7 copy-start.6
  19.1 0.9 copy-start.5
  19.1 1.2 copy-start.9
  413.7 25.2 %copy-start.2 = (f32[3072,2,4,64]{3,2,1,0:T(4,128)S(1)}, f32[3072,2,4,64]{3,2,1,0:T(4,128)}, u32[]{:S(2)}) copy-start(f32[3072,2,4,64]{3,2,1,0:T(4,128)} %reshape_reshape.3) | copy-start | bytes 18874372
  476.8 3.4 copy-start.3
  477.3 2.9 copy-start.4
  481.7 7.8 %copy-start.8 = (bf16[2,128,3072]{2,1,0:T(8,128)(2,1)S(1)}, bf16[2,128,3072]{2,1,0:T(8,128)(2,1)}, u32[]{:S(2)}) copy-start(bf16[2,128,3072]{2,1,0:T(8,128)(2,1)} %param.11) | copy-start | bytes 4718596
  489.5 7.8 %copy-start.7 = (f32[3,128]{1,0:T(4,128)S(1)}, f32[3,128]{1,0:T(4,128)}, u32[]{:S(2)}) copy-start(f32[3,128]{1,0:T(4,128)} %param.12) | copy-start | bytes 4612
  489.5 8.5 %copy-start.1 = (bf16[2,128,3072]{2,1,0:T(8,128)(2,1)S(1)}, bf16[2,128,3072]{2,1,0:T(8,128)(2,1)}, u32[]{:S(2)}) copy-start(bf16[2,128,3072]{2,1,0:T(8,128)(2,1)} %param.10) | copy-start | bytes 4718596
Sparse Core Ops, SparseCore 0:
  19.3 372.8 all-reduce.1
where the time goes:
time: 507 us; the launch traced here: 505 us
  waiting for transfers between devices  362 us (71%)
  matrix products  70.4 us (14%)
  local copies, waits for them, and re-layouts  43.6 us (9%)
  other arithmetic  15.2 us (3%)
  between operations  13.6 us (3%)
    psum x1, waiting for transfers between devices, body(): summed = lax.psum(partial_value, 'band')  362 us
    dot_general x1, matrix products, coefficients(): jnp.einsum('mpa,pab->mpb', weights, pieces[:, 1, 1:], precision=lax.Preci...  25.2 us
    dot_general x1, matrix products, coefficients(): jnp.einsum('mpa,pab->mpb', weights, pieces[:, 0, 1:], precision=lax.Preci...  24.5 us
    another operation x1, local copies, waits for them, and re-layouts, coefficients(): pieces = dcols.reshape(row_count, 2, 4, band_count)  12.3 us
  transfers between devices with their start and end apart: 1, of which 1 were waited for; matrix products, arithmetic and copies ran while one was open for 2% of the time, Pallas kernels for 0%

commit v1 on v0

v1 whole, which is shorter than its diff:
```python
import functools

import jax
import jax.numpy as jnp
from jax import lax
from jax.experimental import pallas as pl
from jax.experimental.pallas import tpu as pltpu
from jax.sharding import PartitionSpec as P

CORES = 2
X = 4
SLOTS = 3
LANES = 128
SEMS = 320


def kernel(
    Z,
    waves,
    kvec,
    beta_k,
    beta_kq_hbm,
    kq,
    dtile,
    sp,
    w,
    out,
    left,
    W,
    CR,
    XA,
    XB,
    ZA,
    ZB,
    G,
    C,
    bkq,
    kq_sem,
    ssem,
    rsem,
):
    half = Z // 2
    me = lax.axis_index("band")
    pb = lax.axis_index("pb")
    c = lax.rem(me, CORES)
    x = lax.rem(lax.div(me, CORES), X)
    z = lax.div(me, CORES * X)
    h = lax.rem(pb, 2)

    def xat(d):
        return lax.rem(x + (X + d), X)

    def zat(d):
        return lax.rem(z + (Z + d), Z)

    def dev(zz, xx, cc):
        return {"band": (zz * X + xx) * CORES + cc}

    other = dev(z, x, 1 - c)
    xr, xl = dev(z, xat(1), c), dev(z, xat(-1), c)
    zr, zl = dev(zat(1), x, c), dev(zat(-1), x, c)
    pair = {"pb": pb + 1 - 2 * h}

    load_kq = pltpu.make_async_copy(beta_kq_hbm, bkq, kq_sem)
    load_kq.start()

    barrier = pltpu.get_barrier_semaphore()
    for who in (other, xr, xl, zr, zl, pair):
        pl.semaphore_signal(barrier, inc=1, device_id=who, device_id_type=pl.DeviceIdType.MESH)

    ids = {}
    pending = []

    def number(key):
        return ids.setdefault(key, len(ids))

    def describe(key, src, dst, who):
        at = number(key)
        return pltpu.make_async_remote_copy(
            src_ref=src,
            dst_ref=dst,
            send_sem=ssem.at[at],
            recv_sem=rsem.at[at],
            device_id=who,
            device_id_type=pl.DeviceIdType.MESH,
        )

    def send(key, src, dst, who):
        copy = describe(key, src, dst, who)
        copy.start()
        pending.append(copy)

    def receive(key, land, who):
        describe(key, land, land, who).wait_recv()

    sre = waves[0].astype(jnp.float32)
    sim = waves[1].astype(jnp.float32)
    bands = sre.shape[0]
    for s in range(4):
        row = 1.0 if s == 0 else kvec[s - 1 : s, :]
        a_part = sre * row
        b_part = sim * row
        rows = pl.ds(s * bands, bands)
        left[rows, 0:LANES] = jnp.where(h == 0, a_part, b_part).astype(jnp.bfloat16)
        left[rows, LANES : 2 * LANES] = jnp.where(h == 0, b_part, -a_part).astype(jnp.bfloat16)

    def product(cc, s, two):
        lanes = pl.multiple_of((cc * SLOTS * X + s * X + two * 2) * LANES, 2 * LANES)
        right = beta_k[:, :, pl.ds(lanes, 2 * LANES)].reshape(2 * LANES, 2 * LANES)
        value = jnp.dot(left[...], right, preferred_element_type=jnp.float32)
        for k in range(2):
            part = value[:, k * LANES : (k + 1) * LANES]
            W[cc, s, 2 * two + k] = part.reshape(W.shape[3:])

    for s in range(SLOTS):
        for two in range(2):
            product(1 - c, s, two)
            if s == 0 and two == 0:
                pl.semaphore_wait(barrier, 6)
            here = pl.ds(2 * two, 2)
            send(("core", s, two), W.at[1 - c, s, here], CR.at[s, here], other)
    for s in range(SLOTS):
        for two in range(2):
            product(c, s, two)

    def x_start(tag, a, b, buf):
        send((tag, 0), a(xat(2)), buf.at[0], xr)
        send((tag, 1), b(xat(2)), buf.at[1], xl)
        send((tag, 2), b(xat(1)), buf.at[2], xr)
        send((tag, 3), a(xat(-1)), buf.at[3], xl)

    def x_middle(tag, a, b, buf):
        receive((tag, 0), buf.at[0], xl)
        a(xat(1))[...] += buf[0]
        send((tag, 4), a(xat(1)), buf.at[4], xr)
        receive((tag, 1), buf.at[1], xr)
        b(xat(-1))[...] += buf[1]
        send((tag, 5), b(xat(-1)), buf.at[5], xl)

    def x_last(tag, a, b, buf):
        receive((tag, 2), buf.at[2], xl)
        receive((tag, 3), buf.at[3], xr)
        receive((tag, 4), buf.at[4], xl)
        receive((tag, 5), buf.at[5], xr)
        a(x)[...] += buf[3] + buf[4]
        b(x)[...] += buf[2] + buf[5]

    def z_send(tag, chunk, buf, k):
        if k < half:
            send((tag, 0, k), chunk(zat(half - k)), buf.at[k], zr)
        if k < half - 1:
            send((tag, 1, k), chunk(zat(k + 1 - half)), buf.at[half + k], zl)

    def z_step(tag, chunk, buf, k):
        if k < half:
            receive((tag, 0, k), buf.at[k], zl)
            chunk(zat(half - 1 - k))[...] += buf[k]
            if k + 1 < half:
                send((tag, 0, k + 1), chunk(zat(half - k - 1)), buf.at[k + 1], zr)
        if k < half - 1:
            receive((tag, 1, k), buf.at[half + k], zr)
            chunk(zat(k + 2 - half))[...] += buf[half + k]
            if k + 1 < half - 1:
                send((tag, 1, k + 1), chunk(zat(k + 2 - half)), buf.at[half + k + 1], zl)

    def a0(t):
        return W.at[c, 0, t, pl.ds(0, half)]

    def b0(t):
        return W.at[c, 0, t, pl.ds(half, half)]

    def a12(t):
        return W.at[c, 1, t, z]

    def b12(t):
        return W.at[c, 2, t, z]

    def chunk0(t):
        return W.at[c, 0, x, t]

    def chunk_of(s):
        return lambda t: W.at[c, s, pl.ds(0, X), t]

    for s in range(SLOTS):
        for two in range(2):
            here = pl.ds(2 * two, 2)
            receive(("core", s, two), CR.at[s, here], other)
            W[c, s, here] += CR[s, here]
        if s == 0:
            x_start("x0", a0, b0, XA)
        else:
            z_send(("z", s), chunk_of(s), ZB.at[s - 1], 0)

    row_atom = lax.broadcasted_iota(jnp.int32, (LANES, LANES), 0) // 8
    lane_atom = lax.broadcasted_iota(jnp.int32, (LANES, LANES), 1) // 8
    same = row_atom == lane_atom

    def mixer(s):
        kinds = sp[pl.ds((c * SLOTS + s) * X + x, 1), :]
        total = jnp.zeros((LANES, LANES), jnp.float32)
        for kind in range(dtile.shape[0]):
            total = jnp.where(same & (kinds == kind), dtile[kind], total)
        return total

    for i in range(half + 3):
        if i < half:
            for s in (1, 2):
                z_step(("z", s), chunk_of(s), ZB.at[s - 1], i)
        if i == 1:
            x_middle("x0", a0, b0, XA)
        if i == 2:
            x_last("x0", a0, b0, XA)
            z_send(("z", 0), chunk0, ZA, 0)
        if i >= 3:
            z_step(("z", 0), chunk0, ZA, i - 3)
        if i == half:
            x_start("x12", a12, b12, XB)
        if i == half + 1:
            x_middle("x12", a12, b12, XB)
        if i == half + 2:
            x_last("x12", a12, b12, XB)

    for s in range(SLOTS):
        G[h, c, s, x, z] = jnp.dot(
            W[c, s, x, z],
            mixer(s),
            precision=lax.Precision.HIGHEST,
            preferred_element_type=jnp.float32,
        )

    both = pl.ds(0, 2)
    three = pl.ds(0, SLOTS)
    four = pl.ds(0, X)
    mine = G.at[h, c, three, x, z]
    send("pair", mine, mine, pair)
    theirs = G.at[1 - h, c, three, x, z]
    receive("pair", theirs, pair)

    def slot_chunk(s):
        return lambda t: G.at[both, c, s, x, t]

    def group_chunk(hh):
        return lambda t: G.at[hh, c, 2, four, t]

    def g_send(tag, chunk, k):
        if k < half:
            send((tag, 0, k), chunk(zat(-k)), chunk(zat(-k)), zr)
        if k < half - 1:
            send((tag, 1, k), chunk(zat(k)), chunk(zat(k)), zl)

    def g_step(tag, chunk, k):
        if k < half:
            land = chunk(zat(-1 - k))
            receive((tag, 0, k), land, zl)
            if k + 1 < half:
                send((tag, 0, k + 1), land, land, zr)
        if k < half - 1:
            land = chunk(zat(k + 1))
            receive((tag, 1, k), land, zr)
            if k + 1 < half - 1:
                send((tag, 1, k + 1), land, land, zl)

    def gx_start(tag, view):
        send((tag, 0), view(both, x), view(both, x), xr)
        send((tag, 1), view(both, x), view(both, x), xl)

    def gx_middle(tag, view):
        receive((tag, 0), view(both, xat(-1)), xl)
        send((tag, 2), view(pl.ds(0, 1), xat(-1)), view(pl.ds(0, 1), xat(-1)), xr)
        receive((tag, 1), view(both, xat(1)), xr)
        send((tag, 3), view(pl.ds(1, 1), xat(1)), view(pl.ds(1, 1), xat(1)), xl)

    def gx_last(tag, view):
        receive((tag, 2), view(pl.ds(0, 1), xat(2)), xl)
        receive((tag, 3), view(pl.ds(1, 1), xat(2)), xr)

    def view01(zz):
        return lambda hh, t: G.at[hh, c, pl.ds(0, 2), t, zz]

    def view2(hh, t):
        return G.at[hh, c, 2, t, z]

    def reached(k):
        if k < 0:
            return [(0, z)]
        found = []
        if k < half:
            found.append((-1 - k, zat(-1 - k)))
        if k < half - 1:
            found.append((k + 1, zat(k + 1)))
        return found

    def to_core(k):
        for d, zz in reached(k):
            block = G.at[both, c, three, four, zz]
            send(("other", d), block, block, other)

    for s in (0, 1):
        g_send(("g", s), slot_chunk(s), 0)
    gx_start("gx2", view2)
    gx_start(("gx", 0), view01(z))
    gx_middle("gx2", view2)
    for i in range(half + 2):
        if i < half:
            for s in (0, 1):
                g_step(("g", s), slot_chunk(s), i)
        if i == 0:
            gx_last("gx2", view2)
            for hh in range(2):
                g_send(("h", hh), group_chunk(hh), 0)
        if i >= 2:
            for hh in range(2):
                g_step(("h", hh), group_chunk(hh), i - 2)
        if i < half:
            for d, zz in reached(i):
                gx_start(("gx", d), view01(zz))
        if i <= half:
            for d, zz in reached(i - 1):
                gx_middle(("gx", d), view01(zz))
        if i >= 1:
            for d, zz in reached(i - 2):
                gx_last(("gx", d), view01(zz))
            to_core(i - 2)
    for k in range(-1, half):
        for d, zz in reached(k):
            receive(("other", d), G.at[both, 1 - c, three, four, zz], other)

    per = bands // (Z // 4)

    def coefficients(n, carry):
        nc = lax.div(n, SLOTS * X)
        ns = lax.rem(lax.div(n, X), SLOTS)
        nx = lax.rem(n, X)
        lanes = pl.ds(pl.multiple_of(n * LANES, LANES), LANES)
        for j in range(Z // 4):
            re = [G[0, nc, ns, nx, s * (Z // 4) + j] for s in range(4)]
            im = [G[1, nc, ns, nx, s * (Z // 4) + j] for s in range(4)]
            for m in range(w.shape[0] // 3):
                ws = [w[3 * m + a : 3 * m + a + 1, lanes] for a in range(3)]
                turned_re = -(ws[0] * im[1] + ws[1] * im[2] + ws[2] * im[3])
                turned_im = ws[0] * re[1] + ws[1] * re[2] + ws[2] * re[3]
                real = [turned_re] + [ws[a] * re[0] for a in range(3)]
                imag = [turned_im] + [ws[a] * im[0] for a in range(3)]
                for t in range(4):
                    at = (m * 8 + t) * bands + j * per
                    C[at : at + per, lanes] = real[t].astype(jnp.bfloat16)
                    at += 4 * bands
                    C[at : at + per, lanes] = imag[t].astype(jnp.bfloat16)
        return carry

    lax.fori_loop(0, CORES * SLOTS * X, coefficients, 0)
    load_kq.wait()

    def back(m, carry):
        rows = pl.ds(pl.multiple_of(m * 8 * bands, 8 * bands), 8 * bands)
        right = bkq[...].reshape(2 * LANES, bkq.shape[2])
        both_parts = lax.dot_general(
            C[rows, :], right, (((1,), (1,)), ((), ())), preferred_element_type=jnp.float32
        )
        top = both_parts[: 4 * bands]
        low = both_parts[4 * bands :]
        back_re = top[:, :LANES] - low[:, LANES:]
        back_im = top[:, LANES:] + low[:, :LANES]
        out_re = back_re[:bands]
        out_im = back_im[:bands]
        for a in range(3):
            rows_a = slice((1 + a) * bands, (2 + a) * bands)
            out_re = out_re + kq[a : a + 1, :] * back_im[rows_a]
            out_im = out_im - kq[a : a + 1, :] * back_re[rows_a]
        out[m, 0] = out_re.astype(jnp.bfloat16)
        out[m, 1] = out_im.astype(jnp.bfloat16)
        return carry

    lax.fori_loop(0, out.shape[0], back, 0)
    for copy in pending:
        copy.wait_send()


def solution(mesh):
    Z = mesh.shape["band"] // (CORES * X)

    def body(waves, kvec, beta_k, beta_kq, kq, d_matrix, species, displacements):
        bands = waves.shape[1]
        projectors = beta_k.shape[2]
        modes = displacements.shape[0]
        per_atom = d_matrix.shape[1]
        per = 4 * bands // Z
        dtile = jnp.tile(d_matrix.transpose(0, 2, 1), (1, LANES // per_atom, LANES // per_atom))
        sp = jnp.repeat(species, per_atom).reshape(projectors // LANES, LANES)
        w = jnp.repeat(displacements.transpose(0, 2, 1).reshape(modes * 3, -1), per_atom, axis=1)
        vmem = pl.BlockSpec(memory_space=pltpu.VMEM)
        f32 = jnp.float32
        return pl.pallas_call(
            functools.partial(kernel, Z),
            out_shape=jax.ShapeDtypeStruct((modes, 2, bands, beta_kq.shape[1]), jnp.bfloat16),
            in_specs=[vmem, vmem, vmem, pl.BlockSpec(memory_space=pl.ANY), vmem, vmem, vmem, vmem],
            out_specs=vmem,
            scratch_shapes=[
                pltpu.VMEM((4 * bands, 2 * LANES), jnp.bfloat16),
                pltpu.VMEM((CORES, SLOTS, X, Z, per, LANES), f32),
                pltpu.VMEM((SLOTS, X, Z, per, LANES), f32),
                pltpu.VMEM((6, Z // 2, per, LANES), f32),
                pltpu.VMEM((6, per, LANES), f32),
                pltpu.VMEM((Z, per, LANES), f32),
                pltpu.VMEM((2, Z, X, per, LANES), f32),
                pltpu.VMEM((2, CORES, SLOTS, X, Z, per, LANES), f32),
                pltpu.VMEM((modes * 8 * bands, projectors), jnp.bfloat16),
                pltpu.VMEM(beta_kq.shape, jnp.bfloat16),
                pltpu.SemaphoreType.DMA,
                pltpu.SemaphoreType.DMA((SEMS,)),
                pltpu.SemaphoreType.DMA((SEMS,)),
            ],
            compiler_params=pltpu.CompilerParams(
                collective_id=0, has_side_effects=True, vmem_limit_bytes=56 * 2**20
            ),
        )(waves, kvec, beta_k, beta_kq, kq, dtile, sp, w)

    in_specs = (
        P(None, None, "band"),
        P(None, "band"),
        P(None, "band", None),
        P(None, ("pb", "band"), None),
        P(None, ("pb", "band")),
        P(),
        P(),
        P("pb", None, None),
    )
    out_specs = P("pb", None, None, "band")
    return jax.shard_map(body, mesh=mesh, in_specs=in_specs, out_specs=out_specs, check_vma=False)
```

time: 507 us -> 131 us (0.26)
  waiting for transfers between devices: 362 us -> 0 us
  Pallas kernels: 0 us -> 118 us
  matrix products: 70.4 us -> 0 us
  local copies, waits for them, and re-layouts: 43.6 us -> 12 us
  other arithmetic: 15.2 us -> 0 us
  between operations: 13.6 us -> 0.03 us
    psum x1 -> x0, waiting for transfers between devices: 362 us -> none  [body(): summed = lax.psum(partial_value, 'band')]
    pallas_call x0 -> x1, Pallas kernels: none -> 118 us  [body(): pl.pallas_call(functools.partial(kernel, Z), out_shape=jax.ShapeDtypeStru...]
    dot_general x6 -> x0, matrix products: 70.4 us -> none  [the longest x1 25.2 us: coefficients(): jnp.einsum('mpa,pab->mpb', weights, pieces[:, 1, 1:], precision=lax.Preci...]
    another operation x7 -> x0, other arithmetic: 12.1 us -> none  [the longest x1 7.77 us: coefficients(): jnp.stack([jnp.concatenate([real_part, imag_part], 1), jnp.concatenate([-...]
    dot_general x3 -> x0, local copies, waits for them, and re-layouts: 7.19 us -> none  [the longest x1 6.54 us: body(): lax.dot_general(beta_k, right, (((0, 1), (0, 2)), ((), ())), preferred_el...]
    broadcast_in_dim x2 -> x5, local copies, waits for them, and re-layouts: 8.36 us -> 1.35 us  [the longest x4 0.84 us: body(): sp = jnp.repeat(species, per_atom).reshape(projectors // LANES, LANES)]
    another operation x1 -> x2, local copies, waits for them, and re-layouts: 12.3 us -> 6.67 us  [body(): jnp.tile(d_matrix.transpose(0, 2, 1), (1, LANES // per_atom, LANES // per...]
  transfers between devices with their start and end apart: 1 -> 0, of which waited for: 1 -> 0; matrix products, arithmetic and copies ran while one was open for 2% -> 0% of each run, Pallas kernels for 0% -> 0%
where the time goes in v1:
time: 131 us; the launch traced here: 130 us
  Pallas kernels  118 us (90%)
  local copies, waits for them, and re-layouts  12 us (9%)
    pallas_call x1, Pallas kernels, body(): pl.pallas_call(functools.partial(kernel, Z), out_shape=jax.ShapeDtypeStru...  118 us
    another operation x2, local copies, waits for them, and re-layouts, body(): jnp.tile(d_matrix.transpose(0, 2, 1), (1, LANES // per_atom, LANES // per...  6.67 us

profile of v1, /device:TPU:33, one launch (start us, length us, event | category | flops | bytes accessed | tf_op | source)
XLA Modules:
  0.0 130.3 jit_solution(4314936387126430226)
XLA Ops:
  0.0 0.8 copy.10
  0.8 2.4 %tile.4 = f32[4,16,8,16,8]{4,3,2,1,0:T(8,128)} broadcast(f32[4,8,8]{2,1,0:T(8,128)S(1)} %copy.10), dimensions={0,2,4} | broadcast | bytes 263168 | tf_op jit(solution)/shard_map/tile | solution.py:388
  3.2 0.0 copy-start
  3.2 4.3 %tile.10.dtile = f32[4,128,128]{2,1,0:T(8,128)} reshape(f32[4,16,8,16,8]{4,3,2,1,0:T(8,128)} %tile.4) | data formatting | bytes 524288 | tf_op jit(solution)/shard_map/tile | solution.py:388
  7.5 0.0 copy-done
  7.5 0.0 copy-start.1
  7.5 0.5 broadcast_in_dim.13
  8.0 1.7 %reshape.13.w = f32[9,3072]{1,0:T(8,128)} reshape(f32[9,384,8]{2,1,0:T(8,128)S(1)} %broadcast_in_dim.13) | data formatting | bytes 221184 | tf_op jit(solution)/shard_map/reshape | solution.py:390
  9.7 0.0 copy-done.1
  9.7 0.1 broadcast_in_dim.10
  9.8 0.1 copy.11
  9.8 0.7 copy.12.sp
  10.5 118.3 %shard_map.82 = bf16[3,2,64,128]{3,2,1,0:T(8,128)(2,1)} custom-call(bf16[2,64,128]{2,1,0:T(8,128)(2,1)} %waves.1, f32[3,128]{1,0:T(4,128)} %kvec.1, bf16[2,128,3072]{2,1,0:T(8,128)(2,1)} %beta_k.1, bf16[2,128,3072]{2,1,0:T(8,128)(2,1)} %beta_kq_hbm.1, f32[3,128]{1,0:T(4,128)} %kq.1, f32[4,128,128]{2,1,0:T(8,128)} %tile.10.dtile, s32[24,128]{1,0:T(8,128)} %copy.12.sp, ...), custom_call_target="tpu_custom_call" | custom-call | tf_op jit(solution)/shard_map/pallas_call | solution.py:393
  128.8 1.5 %copy.14 = bf16[3,2,64,128]{3,2,1,0:T(8,128)(2,1)} copy(bf16[3,2,64,128]{3,2,1,0:T(8,128)(2,1)} %shard_map.82) | data formatting | bytes 196608
  (2 shorter events, 0.0 us)
Async XLA Ops:
  3.2 4.3 %copy-start = (f32[3,384,3]{1,2,0:T(4,128)S(1)}, f32[3,384,3]{1,2,0:T(4,128)}, u32[]{:S(2)}) copy-start(f32[3,384,3]{1,2,0:T(4,128)} %param.15) | copy-start | bytes 41476
  7.5 2.2 %copy-start.1 = (s32[384]{0:T(512)S(1)}, s32[384]{0:T(512)}, u32[]{:S(2)}) copy-start(s32[384]{0:T(512)} %param.14) | copy-start | bytes 4612
